TPU v7x, 32 devices: a whole 2x2x4 slice. The times are simulated.
32 devices in a mesh: groups: 2 (over x), seq: 16 (over z, y, core).
Axes of the slice: x: 2, y: 2, z: 4, core: 2. Of those that a mesh axis runs over, the one named last changes fastest.
Arguments:
- queries: bfloat16 [8192, 4096], P(('groups', 'seq')), parts along dimension 0, may hold values from -6 to 6
- keys: bfloat16 [8192, 2048], P(('groups', 'seq')), parts along dimension 0, may hold values from -6 to 6
- values: bfloat16 [8192, 2048], P(('groups', 'seq')), parts along dimension 0, may hold values from -6 to 6
- doc_blocks: int32 [16], P('groups'), parts along dimension 0, may hold values from 1 to 8, 32 in all
Outputs:
- attended: bfloat16 [8192, 4096], P(('groups', 'seq')), parts along dimension 0
There are 2 independent parts, one for each index of `groups`. A program takes and returns all parts, laid end to end along the dimension named above; each array names one. Nothing has to cross between parts.
Inputs may be any that keep to these rules, and one draw needn't show every extreme that they name: `doc_blocks`: the lengths add up to 32; the longest document has exactly 8 units.
All inputs are finite; a program needn't handle non-finite values.
Results may differ from a plain program's by a relative error of at most 0.004.
Values may be sent and summed in bfloat16 or wider, within the bound.
A program may use at most 64 MiB of HBM per device.

v0:
```python
import jax
import jax.numpy as jnp
from jax import lax
from jax.sharding import PartitionSpec as P

DH = 128
BLK = 128


score_scale = 144.0 ** (-0.5)


def from_partner(block, axis, bit):
    count = lax.axis_size(axis)
    route = []
    for low in range(count):
        high = low | 1 << bit
        if high != low and high < count:
            route += [(low, high), (high, low)]
    return lax.ppermute(block, axis, route)


def attend(
    query_heads, query_pos, all_keys, all_values, key_first, doc_blocks, query_block, key_block
):
    query_rows = query_heads.shape[0]
    key_here = query_heads.shape[1]
    ratio = query_heads.shape[2]
    lengths = doc_blocks * BLK
    doc_ends = jnp.cumsum(lengths)
    doc_starts = doc_ends - lengths
    doc_number = jnp.sum((query_pos[:, None] >= doc_ends[None, :]).astype(jnp.int32), axis=1)
    doc_ids = jnp.arange(doc_blocks.shape[0], dtype=jnp.int32)
    own_start = jnp.sum(
        jnp.where(doc_number[:, None] == doc_ids[None, :], doc_starts[None, :], 0), axis=1
    )

    def one_block(block_index):
        first_row = block_index * query_block
        query_tile = lax.dynamic_slice_in_dim(query_heads, first_row, query_block, 0)
        tile_pos = lax.dynamic_slice_in_dim(query_pos, first_row, query_block, 0)
        tile_start = lax.dynamic_slice_in_dim(own_start, first_row, query_block, 0)
        low_block = (tile_start[0] - key_first) // key_block
        high_block = (tile_pos[query_block - 1] - key_first) // key_block + 1
        state_shape = (key_here, ratio, query_block)
        start_state = (
            jnp.full(state_shape, -1e30, jnp.float32),
            jnp.zeros(state_shape, jnp.float32),
            jnp.zeros(state_shape + (DH,), jnp.float32),
        )

        def key_step(key_index, carried):
            run_max, run_total, run_sum = carried
            key_tile = lax.dynamic_slice_in_dim(all_keys, key_index * key_block, key_block, 0)
            value_tile = lax.dynamic_slice_in_dim(all_values, key_index * key_block, key_block, 0)
            scores = (
                jnp.einsum(
                    "qgsd,kgd->gsqk", query_tile, key_tile, preferred_element_type=jnp.float32
                )
                * score_scale
            )
            key_pos = key_first + key_index * key_block + jnp.arange(key_block, dtype=jnp.int32)
            visible = (key_pos[None, :] >= tile_start[:, None]) & (
                key_pos[None, :] <= tile_pos[:, None]
            )
            masked = jnp.where(visible, scores, -1e30)
            new_max = jnp.maximum(run_max, jnp.max(masked, axis=-1))
            rescale = jnp.exp(run_max - new_max)
            weights = jnp.where(visible, jnp.exp(scores - new_max[..., None]), 0.0)
            run_total = run_total * rescale + jnp.sum(weights, axis=-1)
            run_sum = run_sum * rescale[..., None] + jnp.einsum(
                "gsqk,kgd->gsqd",
                weights.astype(jnp.bfloat16),
                value_tile,
                preferred_element_type=jnp.float32,
            )
            return (new_max, run_total, run_sum)

        finished = lax.fori_loop(low_block, high_block, key_step, start_state)
        blended = finished[2] / finished[1][..., None]
        return (
            blended.transpose(2, 0, 1, 3)
            .reshape(query_block, key_here * ratio * DH)
            .astype(jnp.bfloat16)
        )

    blocks = lax.map(one_block, jnp.arange(query_rows // query_block, dtype=jnp.int32))
    return blocks.reshape(query_rows, key_here * ratio * DH)


def on_device(queries, keys, values, doc_blocks):
    axis_size = lax.axis_size("seq")
    my_index = lax.axis_index("seq")
    shard_rows = queries.shape[0]
    head_count = queries.shape[1] // DH
    key_count = keys.shape[1] // DH
    group_ratio = head_count // key_count
    total_rows = shard_rows * axis_size
    heads_here = max(1, head_count // axis_size)
    row_split = max(1, axis_size // head_count)
    head_groups = head_count // heads_here
    key_here = max(1, heads_here // group_ratio)
    key_groups = key_count // key_here
    copies = axis_size // key_groups
    part_rows = shard_rows // row_split
    query_width = heads_here * DH
    key_width = key_here * DH
    outgoing = queries.reshape(row_split, part_rows, head_groups, query_width).transpose(2, 0, 1, 3)
    outgoing = outgoing.reshape(axis_size, part_rows, query_width)
    got_queries = lax.all_to_all(outgoing, "seq", split_axis=0, concat_axis=0, tiled=True)
    piece_rows = shard_rows // copies
    stacked = jnp.stack((keys, values)).reshape(2, copies, piece_rows, key_groups, key_width)
    stacked = stacked.transpose(0, 3, 1, 2, 4).reshape(2, axis_size, piece_rows, key_width)
    got_pairs = lax.all_to_all(stacked, "seq", split_axis=1, concat_axis=1, tiled=True)
    gathered = got_pairs.reshape(2, axis_size, 1, piece_rows, key_width)
    for bit_number in range(copies.bit_length() - 1):
        partner = from_partner(gathered, "seq", bit_number)
        upper_half = my_index // 2**bit_number % 2 == 1
        gathered = jnp.where(
            upper_half,
            jnp.concatenate((partner, gathered), axis=2),
            jnp.concatenate((gathered, partner), axis=2),
        )
    pairs_flat = gathered.reshape(2, total_rows, key_here, DH)
    all_keys = pairs_flat[0]
    all_values = pairs_flat[1]
    query_rows = total_rows // row_split
    row_ids = jnp.arange(query_rows, dtype=jnp.int32)
    my_part = my_index % row_split
    query_pos = row_ids // part_rows * shard_rows + my_part * part_rows + row_ids % part_rows
    query_heads = got_queries.reshape(query_rows, key_here, heads_here // key_here, DH)
    result = attend(
        query_heads,
        query_pos,
        all_keys,
        all_values,
        0,
        doc_blocks,
        min(512, query_rows),
        min(512, total_rows),
    )
    result_parts = result.reshape(axis_size, part_rows, query_width)
    returned = lax.all_to_all(result_parts, "seq", split_axis=0, concat_axis=0, tiled=True)
    returned = returned.reshape(head_groups, row_split, part_rows, query_width).transpose(
        1, 2, 0, 3
    )
    return returned.reshape(shard_rows, head_count * DH)


def solution(mesh):
    in_specs = (
        P(("groups", "seq"), None),
        P(("groups", "seq"), None),
        P(("groups", "seq"), None),
        P("groups"),
    )
    out_specs = P(("groups", "seq"), None)
    return jax.shard_map(
        on_device, mesh=mesh, in_specs=in_specs, out_specs=out_specs, check_vma=False
    )
```

profile of v0, /device:TPU:1, one launch (start us, length us, event | category | flops | bytes accessed | tf_op | source)
XLA Modules:
  0.0 286.5 jit_solution(64911163191725977)
XLA Ops:
  0.0 4.1 %copy.34 = bf16[256,4096]{0,1:T(8,128)(2,1)} copy(bf16[256,4096]{1,0:T(8,128)(2,1)} %param.8) | data formatting | bytes 4194304 | tf_op args[0]
  4.1 7.3 %all-to-all-start = ((bf16[16,256,256]{1,2,0:T(8,128)(2,1)}), bf16[16,256,256]{1,2,0:T(8,128)(2,1)S(1)}, u32[]{:S(2)}, u32[]{:S(2)}) async-start(bf16[16,256,256]{1,2,0:T(8,128)(2,1)} %bitcast.116), calls=%async_computation | async-start | bytes 4194304 | tf_op jit(solution)/shard_map/all_to_all | solution.py:110
  11.4 1.5 copy.36
  12.9 2.3 copy.37
  15.2 2.8 maximum_bitcast_fusion
  17.9 4.0 %copy.38 = bf16[2,16,256,128]{3,2,0,1:T(8,128)(2,1)} copy(bf16[2,16,256,128]{2,3,1,0:T(8,128)(2,1)} %maximum_bitcast_fusion) | data formatting | bytes 4194304 | tf_op jit(solution)/shard_map/reshape | solution.py:113
  21.9 31.0 %all-to-all-done = bf16[16,256,256]{1,2,0:T(8,128)(2,1)S(1)} async-done(((bf16[16,256,256]{1,2,0:T(8,128)(2,1)}), bf16[16,256,256]{1,2,0:T(8,128)(2,1)S(1)}, u32[]{:S(2)}, u32[]{:S(2)}) %all-to-all-start) | async-done | bytes 2097184 | tf_op jit(solution)/shard_map/all_to_all | solution.py:110
  52.9 10.7 %all-to-all-start.1 = ((bf16[2,16,256,128]{3,2,0,1:T(8,128)(2,1)}), bf16[2,16,256,128]{3,2,0,1:T(8,128)(2,1)}, u32[]{:S(2)}, u32[]{:S(2)}) async-start(bf16[2,16,256,128]{3,2,0,1:T(8,128)(2,1)} %copy.38), calls=%async_computation.1 | async-start | bytes 4194304 | tf_op jit(solution)/shard_map/all_to_all | solution.py:114
  64.1 2.5 copy.35
  66.6 4.2 %reshape.133 = bf16[4096,1,2,128]{0,3,2,1:T(8,128)(2,1)} reshape(bf16[16,256,256]{1,0,2:T(8,128)(2,1)} %copy.35) | data formatting | bytes 4194304 | tf_op jit(solution)/shard_map/reshape | solution.py:131
  70.8 34.5 %all-to-all-done.1 = bf16[2,16,256,128]{3,2,0,1:T(8,128)(2,1)} async-done(((bf16[2,16,256,128]{3,2,0,1:T(8,128)(2,1)}), bf16[2,16,256,128]{3,2,0,1:T(8,128)(2,1)}, u32[]{:S(2)}, u32[]{:S(2)}) %all-to-all-start.1) | async-done | bytes 2097184 | tf_op jit(solution)/shard_map/all_to_all | solution.py:114
  105.2 1.7 fusion.33
  107.0 114.7 %while.44 = (s32[]{:T(128)}, bf16[8,512,256]{2,1,0:T(8,128)(2,1)}, s32[8]{0:T(128)S(1)}, s32[4096]{0:T(1024)S(1)}, s32[4096]{0:T(1024)S(1)}, /*index=5*/bf16[409...) while((s32[]{:T(128)}, bf16[8,512,256]{2,1,0:T(8,128)(2,1)}, ...), condition=%wide.region_8.9_spmd, body=%wide.region_3.8_spmd.sunk | while | flops 275516960 | bytes 12940678 | solution.py:87
  114.5 1.0 constant_dynamic-slice_fusion.2
  115.7 2.3 while.45
  126.8 1.0 constant_dynamic-slice_fusion.2
  128.0 4.5 %while.45 = (s32[]{:T(128)}, f32[1,2,512]{2,1,0:T(2,128)S(1)}, f32[1,2,512]{2,1,0:T(2,128)S(1)}, f32[1,2,512,128]{3,2,1,0:T(8,128)S(1)}, s32[]{:T(128)}, /*index...) while((s32[]{:T(128)}, f32[1,2,512]{2,1,0:T(2,128)S(1)}, ...), condition=%wide.region_7.7_spmd, body=%wide.region_4.6_spmd.sunk | while | flops 275254784 | bytes 8986815 | solution.py:79
  141.4 1.0 constant_dynamic-slice_fusion.2
  142.6 2.3 while.45
  153.8 1.0 constant_dynamic-slice_fusion.2
  155.0 4.5 %while.45 = (s32[]{:T(128)}, f32[1,2,512]{2,1,0:T(2,128)S(1)}, f32[1,2,512]{2,1,0:T(2,128)S(1)}, f32[1,2,512,128]{3,2,1,0:T(8,128)S(1)}, s32[]{:T(128)}, /*index...) while((s32[]{:T(128)}, f32[1,2,512]{2,1,0:T(2,128)S(1)}, ...), condition=%wide.region_7.7_spmd, body=%wide.region_4.6_spmd.sunk | while | flops 275254784 | bytes 8986815 | solution.py:79
  168.4 1.0 constant_dynamic-slice_fusion.2
  169.6 4.5 %while.45 = (s32[]{:T(128)}, f32[1,2,512]{2,1,0:T(2,128)S(1)}, f32[1,2,512]{2,1,0:T(2,128)S(1)}, f32[1,2,512,128]{3,2,1,0:T(8,128)S(1)}, s32[]{:T(128)}, /*index...) while((s32[]{:T(128)}, f32[1,2,512]{2,1,0:T(2,128)S(1)}, ...), condition=%wide.region_7.7_spmd, body=%wide.region_4.6_spmd.sunk | while | flops 275254784 | bytes 8986815 | solution.py:79
  183.0 1.0 constant_dynamic-slice_fusion.2
  184.2 4.5 %while.45 = (s32[]{:T(128)}, f32[1,2,512]{2,1,0:T(2,128)S(1)}, f32[1,2,512]{2,1,0:T(2,128)S(1)}, f32[1,2,512,128]{3,2,1,0:T(8,128)S(1)}, s32[]{:T(128)}, /*index...) while((s32[]{:T(128)}, f32[1,2,512]{2,1,0:T(2,128)S(1)}, ...), condition=%wide.region_7.7_spmd, body=%wide.region_4.6_spmd.sunk | while | flops 275254784 | bytes 8986815 | solution.py:79
  197.6 1.0 constant_dynamic-slice_fusion.2
  198.9 4.5 %while.45 = (s32[]{:T(128)}, f32[1,2,512]{2,1,0:T(2,128)S(1)}, f32[1,2,512]{2,1,0:T(2,128)S(1)}, f32[1,2,512,128]{3,2,1,0:T(8,128)S(1)}, s32[]{:T(128)}, /*index...) while((s32[]{:T(128)}, f32[1,2,512]{2,1,0:T(2,128)S(1)}, ...), condition=%wide.region_7.7_spmd, body=%wide.region_4.6_spmd.sunk | while | flops 275254784 | bytes 8986815 | solution.py:79
  212.3 1.0 constant_dynamic-slice_fusion.2
  213.5 6.8 %while.45 = (s32[]{:T(128)}, f32[1,2,512]{2,1,0:T(2,128)S(1)}, f32[1,2,512]{2,1,0:T(2,128)S(1)}, f32[1,2,512,128]{3,2,1,0:T(8,128)S(1)}, s32[]{:T(128)}, /*index...) while((s32[]{:T(128)}, f32[1,2,512]{2,1,0:T(2,128)S(1)}, ...), condition=%wide.region_7.7_spmd, body=%wide.region_4.6_spmd.sunk | while | flops 275254784 | bytes 8986815 | solution.py:79
  221.7 58.4 %all_to_all.15 = bf16[16,256,256]{2,1,0:T(8,128)(2,1)S(1)} all-to-all(bf16[16,256,256]{2,1,0:T(8,128)(2,1)} %bitcast.121), channel_id=1, replica_groups=mesh['groups'=2,'seq'=16] {'seq'}, dimensions={0} | all-to-all | bytes 4194304 | tf_op jit(solution)/shard_map/all_to_all | solution.py:143
  280.1 2.4 copy.40
  282.4 4.1 %copy.41 = bf16[256,4096]{1,0:T(8,128)(2,1)} copy(bf16[256,4096]{0,1:T(8,128)(2,1)} %bitcast.117) | data formatting | bytes 4194304 | tf_op jit(solution)/shard_map/reshape | solution.py:147
  (234 shorter events, 61.2 us)
Async XLA Ops:
  4.1 48.9 %all-to-all-start = ((bf16[16,256,256]{1,2,0:T(8,128)(2,1)}), bf16[16,256,256]{1,2,0:T(8,128)(2,1)S(1)}, u32[]{:S(2)}, u32[]{:S(2)}) async-start(bf16[16,256,256]{1,2,0:T(8,128)(2,1)} %bitcast.116), calls=%async_computation | async-start | bytes 4194304 | tf_op jit(solution)/shard_map/all_to_all | solution.py:110
  21.9 41.7 %copy-start = (s32[8]{0:T(128)S(1)}, s32[8]{0:T(128)}, u32[]{:S(2)}) copy-start(s32[8]{0:T(128)} %param.11) | copy-start | bytes 100
  52.9 52.3 %all-to-all-start.1 = ((bf16[2,16,256,128]{3,2,0,1:T(8,128)(2,1)}), bf16[2,16,256,128]{3,2,0,1:T(8,128)(2,1)}, u32[]{:S(2)}, u32[]{:S(2)}) async-start(bf16[2,16,256,128]{3,2,0,1:T(8,128)(2,1)} %copy.38), calls=%async_computation.1 | async-start | bytes 4194304 | tf_op jit(solution)/shard_map/all_to_all | solution.py:114
where the time goes:
time: 288 us; the launch traced here: 286 us
  waiting for transfers between devices  65.5 us (23%)
  local copies, waits for them, and re-layouts  60.6 us (21%)
  blocking collectives  58.4 us (20%)
  loops' own time  46.2 us (16%)
  matrix products  20.9 us (7%)
  starting transfers between devices  18 us (6%)
  other arithmetic  16.8 us (6%)
    all_to_all x1, blocking collectives, on_device(): lax.all_to_all(result_parts, 'seq', split_axis=0, concat_axis=0, tiled=True)  58.4 us
    another operation x1, loops' own time, attend(): lax.map(one_block, jnp.arange(query_rows // query_block, dtype=jnp.int32))  45 us
    all_to_all x1, waiting for transfers between devices, on_device(): lax.all_to_all(stacked, 'seq', split_axis=1, concat_axis=1, tiled=True)  34.5 us
    all_to_all x1, waiting for transfers between devices, on_device(): lax.all_to_all(outgoing, 'seq', split_axis=0, concat_axis=0, tiled=True)  31 us
    dot_general x15, matrix products, key_step(): jnp.einsum('gsqk,kgd->gsqd', weights.astype(jnp.bfloat16), value_tile, pr...  12.6 us
    all_to_all x1, starting transfers between devices, on_device(): lax.all_to_all(stacked, 'seq', split_axis=1, concat_axis=1, tiled=True)  10.7 us
    dynamic_slice x16, local copies, waits for them, and re-layouts, one_block(): lax.dynamic_slice_in_dim(query_heads, first_row, query_block, 0)  9.15 us
    dot_general x15, matrix products, key_step(): jnp.einsum('qgsd,kgd->gsqk', query_tile, key_tile, preferred_element_type...  8.27 us
  transfers between devices with their start and end apart: 2, of which 2 were waited for; matrix products, arithmetic and copies ran while one was open for 6% of the time, Pallas kernels for 0%

commit v1 on v0

v1 whole, which is shorter than its diff:
```python
import functools

import jax
import jax.numpy as jnp
from jax import lax
from jax.experimental import pallas as pl
from jax.experimental.pallas import tpu as pltpu
from jax.sharding import PartitionSpec as P

DH = 128
BLK = 128
CHUNK_HEADS = 1
EXP2_SCALE = 144.0 ** (-0.5) * 1.4426950408889634
HIDDEN = -1e30


def kernel(
    n,
    window,
    docs_ref,
    q_hbm,
    k_hbm,
    v_hbm,
    o_hbm,
    q_own,
    k_own,
    v_own,
    k_halo,
    v_halo,
    o_own,
    local_sem,
    out_sem,
    send_sem,
    recv_sem,
):
    me = lax.axis_index("seq")
    pairs = window // 2
    place = lax.rem(me, window)
    base = me - place
    pair = place // 2
    core = lax.rem(me, 2)
    partner = me + 1 - 2 * core
    above = lax.rem(me + window, n)
    below = lax.rem(me + n - window, n)

    rows, kv_width = k_hbm.shape
    ratio = q_hbm.shape[1] // kv_width
    width = CHUNK_HEADS * DH
    chunks = kv_width // width
    blocks = rows // BLK
    own_hbm = (k_hbm, v_hbm)
    halo = (k_halo, v_halo)

    def pair_device(step):
        return base + 2 * lax.rem(pair + step, pairs) + core

    def kv_cols(c):
        return pl.ds(pl.multiple_of(c * width, width), width)

    def q_cols(c):
        return pl.ds(pl.multiple_of(c * width * ratio, width * ratio), width * ratio)

    def remote(c, src_slot, dst_slot, device):
        copies = []
        for kind in range(2):
            if src_slot is None:
                src = own_hbm[kind].at[:, kv_cols(c)]
            else:
                src = halo[kind].at[src_slot, :, kv_cols(c)]
            copies.append(
                pltpu.make_async_remote_copy(
                    src_ref=src,
                    dst_ref=halo[kind].at[dst_slot, :, kv_cols(c)],
                    send_sem=send_sem.at[kind, dst_slot, c],
                    recv_sem=recv_sem.at[kind, dst_slot, c],
                    device_id={"seq": device},
                    device_id_type=pl.DeviceIdType.MESH,
                )
            )
        return copies

    def start(copies):
        for copy in copies:
            copy.start()

    def partner_slot(step):
        return lax.rem(2 * step + 1 - 2 * core + window, window)

    barrier = pltpu.get_barrier_semaphore()
    greet = [above, below, partner] + [pair_device(step) for step in range(1, pairs)]
    for device in greet:
        pl.semaphore_signal(
            barrier, inc=1, device_id={"seq": device}, device_id_type=pl.DeviceIdType.MESH
        )
    local = [
        pltpu.make_async_copy(k_hbm, k_own, local_sem.at[0]),
        pltpu.make_async_copy(v_hbm, v_own, local_sem.at[1]),
        pltpu.make_async_copy(q_hbm, q_own, local_sem.at[2]),
    ]
    start(local)
    pl.semaphore_wait(barrier, len(greet))

    def first_sends(c, carry):
        start(remote(c, None, 0, above))
        for step in range(1, pairs):

            @pl.when(pair + step < pairs)
            def _():
                start(remote(c, None, 2 * step, pair_device(step)))

        @pl.when(core == 0)
        def _():
            start(remote(c, None, 1, partner))

        return carry

    lax.fori_loop(0, chunks, first_sends, 0)

    hide_rows = []
    for a in range(blocks):
        number = me * blocks + a
        end = jnp.int32(0)
        first = jnp.int32(0)
        for d in range(docs_ref.shape[0]):
            end = end + docs_ref[d]
            first = jnp.where(end <= number, end, first)
        held = [(me - window) * blocks + b for b in range(a + 1, blocks)]
        for r in range(1, window):
            held += [(me - r) * blocks + b for b in range(blocks)]
        held += [me * blocks + b for b in range(a + 1)]
        hide_rows.append(
            jnp.concatenate(
                [
                    jnp.full((1, BLK), jnp.where(b >= first, 0.0, HIDDEN), jnp.float32)
                    for b in held
                ],
                axis=1,
            )
        )

    for copy in local:
        copy.wait()

    def attend(c):
        q_index = lax.broadcasted_iota(jnp.int32, (BLK, BLK), 0)
        k_index = lax.broadcasted_iota(jnp.int32, (BLK, BLK), 1)
        causal = jnp.where(k_index <= q_index, 0.0, HIDDEN).astype(jnp.float32)
        causal = jnp.concatenate([causal] * ratio, axis=0)
        for h in range(CHUNK_HEADS):
            cols = pl.ds(pl.multiple_of(c * width + h * DH, DH), DH)
            for a in range(blocks):
                own_rows = (a + 1) * BLK

                def gathered(halo_ref, own_ref):
                    parts = []
                    if own_rows < rows:
                        parts.append(halo_ref[0, own_rows:, cols])
                    for r in range(1, window):
                        parts.append(halo_ref[r, :, cols])
                    parts.append(own_ref[:own_rows, cols])
                    return jnp.concatenate(parts, axis=0)

                head_cols = [
                    pl.ds(pl.multiple_of((c * width + h * DH) * ratio + g * DH, DH), DH)
                    for g in range(ratio)
                ]
                tile_rows = slice(a * BLK, (a + 1) * BLK)
                q_tile = jnp.concatenate([q_own[tile_rows, hc] for hc in head_cols], axis=0)
                scores = lax.dot_general(
                    q_tile,
                    gathered(k_halo, k_own),
                    (((1,), (1,)), ((), ())),
                    preferred_element_type=jnp.float32,
                )
                scores = scores + hide_rows[a]
                scores = jnp.concatenate([scores[:, :-BLK], scores[:, -BLK:] + causal], axis=1)
                top = jnp.max(scores, axis=1, keepdims=True)
                weights = jnp.exp2((scores - top) * EXP2_SCALE)
                total = jnp.sum(weights, axis=1, keepdims=True)
                blended = jnp.dot(
                    weights.astype(jnp.bfloat16),
                    gathered(v_halo, v_own),
                    preferred_element_type=jnp.float32,
                )
                blended = (blended / total).astype(o_own.dtype)
                for g in range(ratio):
                    o_own[tile_rows, head_cols[g]] = blended[g * BLK : (g + 1) * BLK]

    def out_copy(c):
        return pltpu.make_async_copy(o_own.at[:, q_cols(c)], o_hbm.at[:, q_cols(c)], out_sem.at[c])

    def arrived(c, slot):
        for copy in remote(c, None, slot, partner):
            copy.wait_recv()

    def step_of(t, carry):
        @pl.when(t < chunks)
        def _():
            c = t
            arrived(c, 0)

            @pl.when(core == 1)
            def _():
                start(remote(c, 0, window - 1, partner))

            for step in range(1, pairs):

                @pl.when(pair + step >= pairs)
                def _():
                    start(remote(c, 0, 2 * step, pair_device(step)))

        @pl.when((t >= 1) & (t < chunks + 1))
        def _():
            c = t - 1
            for step in range(1, pairs):
                arrived(c, 2 * step)
                start(remote(c, 2 * step, partner_slot(step), partner))

        @pl.when((t >= 2) & (t < chunks + 2))
        def _():
            c = t - 2
            for r in range(1, window, 2):
                arrived(c, r)
            attend(c)

        @pl.when(t >= 3)
        def _():
            out_copy(t - 3).start()

        return carry

    lax.fori_loop(0, chunks + 3, step_of, 0)

    def finish(c, carry):
        for slot in range(window):
            for copy in remote(c, None, slot, partner):
                copy.wait_send()
        out_copy(c).wait()
        return carry

    lax.fori_loop(0, chunks, finish, 0)


def on_device(n, queries, keys, values, doc_blocks):
    window = n // 4
    rows, kv_width = keys.shape
    chunks = kv_width // (CHUNK_HEADS * DH)
    return pl.pallas_call(
        functools.partial(kernel, n, window),
        out_shape=jax.ShapeDtypeStruct(queries.shape, queries.dtype),
        in_specs=[pl.BlockSpec(memory_space=pltpu.SMEM)]
        + [pl.BlockSpec(memory_space=pl.ANY)] * 3,
        out_specs=pl.BlockSpec(memory_space=pl.ANY),
        scratch_shapes=[
            pltpu.VMEM(queries.shape, queries.dtype),
            pltpu.VMEM(keys.shape, keys.dtype),
            pltpu.VMEM(values.shape, values.dtype),
            pltpu.VMEM((window, rows, kv_width), keys.dtype),
            pltpu.VMEM((window, rows, kv_width), values.dtype),
            pltpu.VMEM(queries.shape, queries.dtype),
            pltpu.SemaphoreType.DMA((3,)),
            pltpu.SemaphoreType.DMA((chunks,)),
            pltpu.SemaphoreType.DMA((2, window, chunks)),
            pltpu.SemaphoreType.DMA((2, window, chunks)),
        ],
        compiler_params=pltpu.CompilerParams(
            collective_id=0, has_side_effects=True, vmem_limit_bytes=60 * 1024 * 1024
        ),
    )(doc_blocks, queries, keys, values)


def solution(mesh):
    spread = P(("groups", "seq"), None)
    return jax.shard_map(
        functools.partial(on_device, mesh.shape["seq"]),
        mesh=mesh,
        in_specs=(spread, spread, spread, P("groups")),
        out_specs=spread,
        check_vma=False,
    )
```

time: 288 us -> 66.4 us (0.23)
  waiting for transfers between devices: 65.5 us -> 0 us
  Pallas kernels: 0 us -> 62.7 us
  blocking collectives: 58.4 us -> 0 us
  local copies, waits for them, and re-layouts: 60.6 us -> 3.13 us
  loops' own time: 46.2 us -> 0 us
  matrix products: 20.9 us -> 0 us
  starting transfers between devices: 18 us -> 0 us
  other arithmetic: 16.8 us -> 0 us
    all_to_all x2 -> x0, waiting for transfers between devices: 65.5 us -> none  [the longest x1 34.5 us: on_device(): lax.all_to_all(stacked, 'seq', split_axis=1, concat_axis=1, tiled=True)]
    pallas_call x0 -> x1, Pallas kernels: none -> 62.7 us  [on_device(): pl.pallas_call(functools.partial(kernel, n, window), out_shape=jax.ShapeD...]
    all_to_all x1 -> x0, blocking collectives: 58.4 us -> none  [on_device(): lax.all_to_all(result_parts, 'seq', split_axis=0, concat_axis=0, tiled=True)]
    another operation x9 -> x0, loops' own time: 46.2 us -> none  [the longest x1 45 us: attend(): lax.map(one_block, jnp.arange(query_rows // query_block, dtype=jnp.int32))]
    dot_general x30 -> x0, matrix products: 20.9 us -> none  [the longest x15 12.6 us: key_step(): jnp.einsum('gsqk,kgd->gsqd', weights.astype(jnp.bfloat16), value_tile, pr...]
    all_to_all x2 -> x0, starting transfers between devices: 18 us -> none  [the longest x1 10.7 us: on_device(): lax.all_to_all(stacked, 'seq', split_axis=1, concat_axis=1, tiled=True)]
    dynamic_slice x40 -> x0, local copies, waits for them, and re-layouts: 15.2 us -> none  [the longest x16 9.15 us: one_block(): lax.dynamic_slice_in_dim(query_heads, first_row, query_block, 0)]
    reshape x3 -> x0, local copies, waits for them, and re-layouts: 12.2 us -> none  [the longest x1 4.2 us: on_device(): got_queries.reshape(query_rows, key_here, heads_here // key_here, DH)]
  transfers between devices with their start and end apart: 2 -> 0, of which waited for: 2 -> 0; matrix products, arithmetic and copies ran while one was open for 6% -> 0% of each run, Pallas kernels for 0% -> 0%
where the time goes in v1:
time: 66.4 us; the launch traced here: 65.8 us
  Pallas kernels  62.7 us (94%)
  local copies, waits for them, and re-layouts  3.13 us (5%)
    pallas_call x1, Pallas kernels, on_device(): pl.pallas_call(functools.partial(kernel, n, window), out_shape=jax.ShapeD...  62.7 us
    unnamed x1, local copies, waits for them, and re-layouts  3.13 us

profile of v1, /device:TPU:1, one launch (start us, length us, event | category | flops | bytes accessed | tf_op | source)
XLA Modules:
  0.0 65.8 jit_solution(9657596860245399664)
XLA Ops:
  0.0 62.7 %shard_map.46 = bf16[256,4096]{1,0:T(8,128)(2,1)} custom-call(s32[8]{0:T(128)} %docs_ref.1, bf16[256,4096]{1,0:T(8,128)(2,1)} %q_hbm.1, bf16[256,2048]{1,0:T(8,128)(2,1)} %k_hbm.1, bf16[256,2048]{1,0:T(8,128)(2,1)} %v_hbm.1), custom_call_target="tpu_custom_call" | custom-call | tf_op jit(solution)/shard_map/pallas_call | solution.py:248
  62.7 3.1 %copy.6 = bf16[256,4096]{1,0:T(8,128)(2,1)} copy(bf16[256,4096]{1,0:T(8,128)(2,1)} %shard_map.46) | data formatting | bytes 4194304

commit v2 on v1

--- a/solution.py
+++ b/solution.py
@@ -10,6 +10,7 @@
 DH = 128
 BLK = 128
 CHUNK_HEADS = 1
+ROUTED = 1
 EXP2_SCALE = 144.0 ** (-0.5) * 1.4426950408889634
 HIDDEN = -1e30
 
@@ -21,17 +22,20 @@
     q_hbm,
     k_hbm,
     v_hbm,
-    o_hbm,
+    o_own,
     q_own,
     k_own,
     v_own,
     k_halo,
     v_halo,
-    o_own,
     local_sem,
-    out_sem,
     send_sem,
     recv_sem,
+    k_transit,
+    v_transit,
+    transit_send,
+    transit_recv,
+    forward_send,
 ):
     me = lax.axis_index("seq")
     pairs = window // 2
@@ -40,8 +44,10 @@
     pair = place // 2
     core = lax.rem(me, 2)
     partner = me + 1 - 2 * core
-    above = lax.rem(me + window, n)
-    below = lax.rem(me + n - window, n)
+    above = me + window
+    below = me - window
+    has_above = above < n
+    has_below = below >= 0
 
     rows, kv_width = k_hbm.shape
     ratio = q_hbm.shape[1] // kv_width
@@ -50,6 +56,8 @@
     blocks = rows // BLK
     own_hbm = (k_hbm, v_hbm)
     halo = (k_halo, v_halo)
+    transit = (k_transit, v_transit)
+    first_routed = chunks - ROUTED
 
     def pair_device(step):
         return base + 2 * lax.rem(pair + step, pairs) + core
@@ -57,27 +65,61 @@
     def kv_cols(c):
         return pl.ds(pl.multiple_of(c * width, width), width)
 
-    def q_cols(c):
-        return pl.ds(pl.multiple_of(c * width * ratio, width * ratio), width * ratio)
+    def remote_one(kind, c, src_slot, dst_slot, device, from_row=0):
+        taken = pl.ds(from_row, rows - from_row)
+        if src_slot is None:
+            src = own_hbm[kind].at[taken, kv_cols(c)]
+        else:
+            src = halo[kind].at[src_slot, taken, kv_cols(c)]
+        return pltpu.make_async_remote_copy(
+            src_ref=src,
+            dst_ref=halo[kind].at[dst_slot, taken, kv_cols(c)],
+            send_sem=send_sem.at[kind, dst_slot, c],
+            recv_sem=recv_sem.at[kind, dst_slot, c],
+            device_id={"seq": device},
+            device_id_type=pl.DeviceIdType.MESH,
+        )
+
+    def is_routed(c):
+        return (c >= first_routed) & (c < first_routed + ROUTED)
+
+    def turn(spot):
+        moved = jnp.where(spot < chunks - 1, spot + 1, first_routed - 1)
+        return jnp.where((pair == 0) & (spot >= first_routed - 1), moved, spot)
+
+    def across(kind, c, step):
+        spot = c - first_routed
+        return pltpu.make_async_remote_copy(
+            src_ref=own_hbm[kind].at[:, kv_cols(c)],
+            dst_ref=transit[kind].at[step - 1, spot],
+            send_sem=transit_send.at[kind, step - 1, spot],
+            recv_sem=transit_recv.at[kind, step - 1, spot],
+            device_id={"seq": pair_device(step)},
+            device_id_type=pl.DeviceIdType.MESH,
+        )
+
+    def forward(kind, c, step):
+        spot = c - first_routed
+        return pltpu.make_async_remote_copy(
+            src_ref=transit[kind].at[step - 1, spot],
+            dst_ref=halo[kind].at[2 * step, :, kv_cols(c)],
+            send_sem=forward_send.at[kind, step - 1, spot],
+            recv_sem=recv_sem.at[kind, 2 * step, c],
+            device_id={"seq": above},
+            device_id_type=pl.DeviceIdType.MESH,
+        )
 
     def remote(c, src_slot, dst_slot, device):
-        copies = []
-        for kind in range(2):
-            if src_slot is None:
-                src = own_hbm[kind].at[:, kv_cols(c)]
-            else:
-                src = halo[kind].at[src_slot, :, kv_cols(c)]
-            copies.append(
-                pltpu.make_async_remote_copy(
-                    src_ref=src,
-                    dst_ref=halo[kind].at[dst_slot, :, kv_cols(c)],
-                    send_sem=send_sem.at[kind, dst_slot, c],
-                    recv_sem=recv_sem.at[kind, dst_slot, c],
-                    device_id={"seq": device},
-                    device_id_type=pl.DeviceIdType.MESH,
-                )
-            )
-        return copies
+        return [remote_one(kind, c, src_slot, dst_slot, device) for kind in range(2)]
+
+    def upward(kind, c, act):
+        @pl.when(place == 0)
+        def _():
+            act(remote_one(kind, c, None, 0, above, BLK))
+
+        @pl.when(place != 0)
+        def _():
+            act(remote_one(kind, c, None, 0, above))
 
     def start(copies):
         for copy in copies:
@@ -87,21 +129,52 @@
         return lax.rem(2 * step + 1 - 2 * core + window, window)
 
     barrier = pltpu.get_barrier_semaphore()
-    greet = [above, below, partner] + [pair_device(step) for step in range(1, pairs)]
-    for device in greet:
+
+    def greet(device):
         pl.semaphore_signal(
             barrier, inc=1, device_id={"seq": device}, device_id_type=pl.DeviceIdType.MESH
         )
+
+    greet(partner)
+    for step in range(1, pairs):
+        greet(pair_device(step))
+
+    @pl.when(has_above)
+    def _():
+        greet(above)
+
+    @pl.when(has_below)
+    def _():
+        greet(below)
+
     local = [
         pltpu.make_async_copy(k_hbm, k_own, local_sem.at[0]),
         pltpu.make_async_copy(v_hbm, v_own, local_sem.at[1]),
         pltpu.make_async_copy(q_hbm, q_own, local_sem.at[2]),
     ]
     start(local)
-    pl.semaphore_wait(barrier, len(greet))
+    pl.semaphore_wait(
+        barrier, pairs + has_above.astype(jnp.int32) + has_below.astype(jnp.int32)
+    )
+
+    def cross_first(spot, carry):
+        for step in range(1, pairs):
+
+            @pl.when((pair + step >= pairs) & has_above)
+            def _():
+                for kind in range(2):
+                    across(kind, first_routed + spot, step).start()
+
+        return carry
+
+    lax.fori_loop(0, ROUTED, cross_first, 0)
 
     def first_sends(c, carry):
-        start(remote(c, None, 0, above))
+        @pl.when(has_above)
+        def _():
+            for kind in range(2):
+                upward(kind, c, lambda copy: copy.start())
+
         for step in range(1, pairs):
 
             @pl.when(pair + step < pairs)
@@ -115,6 +188,20 @@
         return carry
 
     lax.fori_loop(0, chunks, first_sends, 0)
+
+    @pl.when(jnp.logical_not(has_below))
+    def _():
+        for r in range(window):
+
+            @pl.when((r == 0) | (r > place))
+            def _():
+                def clear(i, carry):
+                    taken = pl.ds(pl.multiple_of(i * 16, 16), 16)
+                    for ref in halo:
+                        ref[r, taken, :] = jnp.zeros((16, kv_width), ref.dtype)
+                    return carry
+
+                lax.fori_loop(0, rows // 16, clear, 0)
 
     hide_rows = []
     for a in range(blocks):
@@ -186,56 +273,97 @@
                 for g in range(ratio):
                     o_own[tile_rows, head_cols[g]] = blended[g * BLK : (g + 1) * BLK]
 
-    def out_copy(c):
-        return pltpu.make_async_copy(o_own.at[:, q_cols(c)], o_hbm.at[:, q_cols(c)], out_sem.at[c])
-
     def arrived(c, slot):
         for copy in remote(c, None, slot, partner):
             copy.wait_recv()
 
     def step_of(t, carry):
-        @pl.when(t < chunks)
+        @pl.when((t < chunks) & has_below)
         def _():
             c = t
-            arrived(c, 0)
-
-            @pl.when(core == 1)
-            def _():
-                start(remote(c, 0, window - 1, partner))
-
+            for kind in range(2):
+                upward(kind, c, lambda copy: copy.wait_recv())
+
+                @pl.when(core == 1)
+                def _():
+                    remote_one(kind, c, 0, window - 1, partner).start()
+
+                for step in range(1, pairs):
+
+                    @pl.when((pair + step >= pairs) & jnp.logical_not(is_routed(c)))
+                    def _():
+                        remote_one(kind, c, 0, 2 * step, pair_device(step)).start()
+
+        @pl.when((t < ROUTED) & has_above)
+        def _():
             for step in range(1, pairs):
 
-                @pl.when(pair + step >= pairs)
+                @pl.when(step > pair)
                 def _():
-                    start(remote(c, 0, 2 * step, pair_device(step)))
+                    for kind in range(2):
+                        across(kind, t + first_routed, step).wait_recv()
+                        forward(kind, t + first_routed, step).start()
 
         @pl.when((t >= 1) & (t < chunks + 1))
         def _():
-            c = t - 1
+            c = turn(t - 1)
             for step in range(1, pairs):
-                arrived(c, 2 * step)
-                start(remote(c, 2 * step, partner_slot(step), partner))
+
+                @pl.when((pair >= step) | has_below)
+                def _():
+                    for kind in range(2):
+                        remote_one(kind, c, None, 2 * step, partner).wait_recv()
+                        remote_one(kind, c, 2 * step, partner_slot(step), partner).start()
 
         @pl.when((t >= 2) & (t < chunks + 2))
         def _():
-            c = t - 2
+            c = turn(t - 2)
             for r in range(1, window, 2):
-                arrived(c, r)
+
+                @pl.when((place >= r) | has_below)
+                def _():
+                    arrived(c, r)
+
             attend(c)
 
-        @pl.when(t >= 3)
-        def _():
-            out_copy(t - 3).start()
-
         return carry
 
-    lax.fori_loop(0, chunks + 3, step_of, 0)
+    lax.fori_loop(0, chunks + 2, step_of, 0)
 
     def finish(c, carry):
-        for slot in range(window):
+        def sent(slot):
             for copy in remote(c, None, slot, partner):
                 copy.wait_send()
-        out_copy(c).wait()
+
+        @pl.when(has_above)
+        def _():
+            for kind in range(2):
+                upward(kind, c, lambda copy: copy.wait_send())
+
+        @pl.when((core == 0) | has_below)
+        def _():
+            sent(partner_slot(0))
+
+        for step in range(1, pairs):
+
+            @pl.when((pair + step < pairs) | (has_below & jnp.logical_not(is_routed(c))))
+            def _():
+                sent(2 * step)
+
+            @pl.when((pair + step >= pairs) & has_above & is_routed(c))
+            def _():
+                for kind in range(2):
+                    across(kind, c, step).wait_send()
+
+            @pl.when((step > pair) & has_above & is_routed(c))
+            def _():
+                for kind in range(2):
+                    forward(kind, c, step).wait_send()
+
+            @pl.when((pair >= step) | has_below)
+            def _():
+                sent(partner_slot(step))
+
         return carry
 
     lax.fori_loop(0, chunks, finish, 0)
@@ -247,21 +375,24 @@
     chunks = kv_width // (CHUNK_HEADS * DH)
     return pl.pallas_call(
         functools.partial(kernel, n, window),
-        out_shape=jax.ShapeDtypeStruct(queries.shape, queries.dtype),
+        out_shape=pltpu.VMEM(queries.shape, queries.dtype),
         in_specs=[pl.BlockSpec(memory_space=pltpu.SMEM)]
         + [pl.BlockSpec(memory_space=pl.ANY)] * 3,
-        out_specs=pl.BlockSpec(memory_space=pl.ANY),
+        out_specs=pl.BlockSpec(memory_space=pltpu.VMEM),
         scratch_shapes=[
             pltpu.VMEM(queries.shape, queries.dtype),
             pltpu.VMEM(keys.shape, keys.dtype),
             pltpu.VMEM(values.shape, values.dtype),
             pltpu.VMEM((window, rows, kv_width), keys.dtype),
             pltpu.VMEM((window, rows, kv_width), values.dtype),
-            pltpu.VMEM(queries.shape, queries.dtype),
             pltpu.SemaphoreType.DMA((3,)),
-            pltpu.SemaphoreType.DMA((chunks,)),
             pltpu.SemaphoreType.DMA((2, window, chunks)),
             pltpu.SemaphoreType.DMA((2, window, chunks)),
+            pltpu.VMEM((window // 2 - 1, ROUTED, rows, CHUNK_HEADS * DH), keys.dtype),
+            pltpu.VMEM((window // 2 - 1, ROUTED, rows, CHUNK_HEADS * DH), values.dtype),
+            pltpu.SemaphoreType.DMA((2, window // 2 - 1, ROUTED)),
+            pltpu.SemaphoreType.DMA((2, window // 2 - 1, ROUTED)),
+            pltpu.SemaphoreType.DMA((2, window // 2 - 1, ROUTED)),
         ],
         compiler_params=pltpu.CompilerParams(
             collective_id=0, has_side_effects=True, vmem_limit_bytes=60 * 1024 * 1024

time: 66.4 us -> 58 us (0.87)
  the two profiles are of different devices: /device:TPU:1 before, /device:TPU:17 now
where the time goes in v2:
time: 58 us; the launch traced here: 57.9 us
  Pallas kernels  56.5 us (97%)
  local copies, waits for them, and re-layouts  1.32 us (2%)
    pallas_call x1, Pallas kernels, on_device(): pl.pallas_call(functools.partial(kernel, n, window), out_shape=pltpu.VMEM...  56.5 us
    unnamed x1, local copies, waits for them, and re-layouts  1.32 us

profile of v2, /device:TPU:17, one launch (start us, length us, event | category | flops | bytes accessed | tf_op | source)
XLA Modules:
  0.0 57.9 jit_solution(7924626519961433234)
XLA Ops:
  0.0 56.5 %shard_map.46 = bf16[256,4096]{1,0:T(8,128)(2,1)S(1)} custom-call(s32[8]{0:T(128)} %docs_ref.1, bf16[256,4096]{1,0:T(8,128)(2,1)} %q_hbm.1, bf16[256,2048]{1,0:T(8,128)(2,1)} %k_hbm.1, bf16[256,2048]{1,0:T(8,128)(2,1)} %v_hbm.1), custom_call_target="tpu_custom_call" | custom-call | tf_op jit(solution)/shard_map/pallas_call | solution.py:376
  56.5 1.3 %copy.6 = bf16[256,4096]{1,0:T(8,128)(2,1)} copy(bf16[256,4096]{1,0:T(8,128)(2,1)S(1)} %shard_map.46) | data formatting | bytes 4194304
